TPU v7x, 256 devices: a whole 4x4x8 slice. The times are simulated.
256 devices in a mesh: blk: 128 (over x, z, y), row: 2 (over core).
Axes of the slice: x: 4, y: 4, z: 8, core: 2. Of those that a mesh axis runs over, the one named last changes fastest.
Arguments:
- genotypes: bfloat16 [1024, 128, 2048], P('blk', None, 'row'), may hold values from 0 to 2
- assignment: int32 [128], replicated, may hold values from 0 to 127, each once
- snp_counts: int32 [128], replicated, may hold values from 1024 to 2048, as said below
- basis: float32 [128, 64, 2048], P('blk', None, 'row'), may hold values from -6 to 6
Outputs:
- image: float32 [128, 64, 2048], P('blk', None, 'row')
- new_basis: float32 [128, 64, 2048], P('blk', None, 'row')
- factor: float32 [128, 64, 64], P('blk')
Inputs may be any that keep to these rules, and one draw needn't show every extreme that they name: `assignment`: each block number appears exactly once. `snp_counts`: A block's SNPs fill its leading slots.
All inputs are finite; a program needn't handle non-finite values.
Results may differ from a plain program's by a relative error of at most 0.0021.
Values may be sent and summed in bfloat16 or wider, within the bound.
A program may use at most 64 MiB of HBM per device.

v0:
```python
import jax
import jax.numpy as jnp
from jax import lax
from jax.sharding import PartitionSpec as P

epsilon = 1e-05
shrink_weight = 0.5


def total_of_pieces(array, axis):
    pieces = lax.all_gather(array, axis)
    return pieces.sum(axis=0)


def body(genotypes, assignment, snp_counts, basis):
    ordered = jnp.take(genotypes, assignment, axis=1)
    regrouped = lax.all_to_all(ordered, "blk", split_axis=1, concat_axis=0, tiled=True)
    samples = regrouped.shape[0]
    owned = regrouped.shape[1]
    half_width = regrouped.shape[2]
    block_ids = lax.dynamic_slice_in_dim(assignment, lax.axis_index("blk") * owned, owned)
    catalog = jnp.arange(snp_counts.shape[0], dtype=jnp.int32)
    live_count = jnp.sum(
        jnp.where(block_ids[:, None] == catalog[None, :], snp_counts[None, :], 0), axis=1
    )
    columns = lax.axis_index("row") * half_width + jnp.arange(half_width, dtype=jnp.int32)
    live_mask = columns[None, :] < live_count[:, None]
    values = regrouped.astype(jnp.float32)
    col_mean = jnp.mean(values, axis=0)
    centered = values - col_mean[None]
    col_var = jnp.mean(centered * centered, axis=0)
    standard = jnp.where(
        live_mask[None], centered * lax.rsqrt(col_var + epsilon)[None], 0.0
    ).astype(jnp.bfloat16)
    inverse = 1.0 / samples
    partial_proj = jnp.einsum(
        "nbi,bri->brn",
        standard,
        basis,
        precision=lax.Precision.HIGHEST,
        preferred_element_type=jnp.float32,
    )
    projected = total_of_pieces(partial_proj, "row")
    product = (
        jnp.einsum(
            "nbi,brn->bri",
            standard,
            projected,
            precision=lax.Precision.HIGHEST,
            preferred_element_type=jnp.float32,
        )
        * inverse
    )
    image = shrink_weight * product + (1.0 - shrink_weight) * jnp.where(
        live_mask[:, None, :], basis, 0.0
    )
    gram_part = jnp.einsum("bri,bsi->brs", image, image, precision=lax.Precision.HIGHEST)
    gram_sum = total_of_pieces(gram_part, "row")
    factor = jnp.linalg.cholesky(gram_sum)
    new_basis = jax.scipy.linalg.solve_triangular(factor, image, lower=True)
    return (image, new_basis, factor)


def solution(mesh):
    in_specs = (P("blk", None, "row"), P(), P(), P("blk", None, "row"))
    out_specs = (P("blk", None, "row"), P("blk", None, "row"), P("blk", None, None))
    return jax.shard_map(body, mesh=mesh, in_specs=in_specs, out_specs=out_specs, check_vma=False)
```

profile of v0, /device:TPU:1, one launch (start us, length us, event | category | flops | bytes accessed | tf_op | source)
XLA Modules:
  0.0 113.4 jit_solution(6416810635120617516)
XLA Ops:
  0.6 0.0 copy-start
  0.6 0.8 compare_select_fusion
  1.5 0.7 compare_and_fusion
  2.1 0.1 copy-done
  2.2 8.1 %gather_fusion = bf16[128,8,1024]{2,0,1:T(8,128)(2,1)} fusion(bf16[8,128,1024]{2,1,0:T(8,128)(2,1)S(1)} %copy-done, s32[1024]{0:T(1024)S(1)} %pad_clamp_fusion), kind=kCustom, calls=%fused_computation | custom fusion | bytes 4194816 | tf_op jit(solution)/shard_map/jit(_take)/gather | solution.py:16
  10.3 1.8 %select_bitcast_fusion = bf16[8,128,1024]{2,1,0:T(8,128)(2,1)S(1)} fusion(bf16[128,8,1024]{2,0,1:T(8,128)(2,1)} %gather_fusion, pred[128]{0:T(512)(128)(4,1)S(1)} %compare_and_fusion), kind=kLoop, calls=%fused_computation.18 | loop fusion | flops 1048576 | bytes 4194432 | tf_op jit(solution)/shard_map/jit(_take)/select_n | solution.py:16
  12.1 2.4 %copy.12 = bf16[8,128,1024]{2,0,1:T(8,128)(2,1)} copy(bf16[8,128,1024]{2,1,0:T(8,128)(2,1)S(1)} %select_bitcast_fusion) | data formatting | bytes 4194304 | tf_op jit(solution)/shard_map/jit(_take)/select_n | solution.py:16
  14.6 0.0 copy-start.3
  14.6 0.0 copy-start.4
  14.6 17.2 %all-to-all-start = ((bf16[8,128,1024]{2,0,1:T(8,128)(2,1)}), bf16[8,128,1024]{2,0,1:T(8,128)(2,1)}, u32[]{:S(2)}, u32[]{:S(2)}) async-start(bf16[8,128,1024]{2,0,1:T(8,128)(2,1)} %copy.12), calls=%async_computation | async-start | bytes 4194304 | tf_op jit(solution)/shard_map/all_to_all | solution.py:17
  31.8 0.0 copy-done.3
  31.8 0.6 dynamic_slice.3
  32.4 0.0 copy-done.4
  32.4 1.3 %fusion.40 = s32[]{:T(128)} fusion(s32[128]{0:T(128)S(1)} %copy-done.4, s32[]{:T(128)} %bitcast), kind=kLoop, calls=%fused_computation.50 | loop fusion | flops 383 | bytes 520 | tf_op jit(solution)/shard_map/reduce_sum | solution.py:23
  33.7 0.7 add_compare_fusion
  34.3 0.0 copy-start.2
  34.3 46.3 %all-to-all-done = bf16[8,128,1024]{2,0,1:T(8,128)(2,1)} async-done(((bf16[8,128,1024]{2,0,1:T(8,128)(2,1)}), bf16[8,128,1024]{2,0,1:T(8,128)(2,1)}, u32[]{:S(2)}, u32[]{:S(2)}) %all-to-all-start) | async-done | bytes 2097184 | tf_op jit(solution)/shard_map/all_to_all | solution.py:17
  80.6 2.0 %convert_reduce_fusion = f32[1024]{0:T(1024)S(1)} fusion(bf16[8,128,1024]{2,0,1:T(8,128)(2,1)} %all-to-all-done), kind=kLoop, calls=%fused_computation.3 | loop fusion | flops 2096128 | bytes 2101248 | tf_op jit(solution)/shard_map/reduce_sum | solution.py:29
  82.6 2.2 %fusion.10 = f32[1024]{0:T(1024)S(1)} fusion(bf16[8,128,1024]{2,0,1:T(8,128)(2,1)} %all-to-all-done, f32[1024]{0:T(1024)S(1)} %broadcast_multiply_fusion), kind=kLoop, calls=%fused_computation.15 | loop fusion | flops 4193280 | bytes 2105344 | tf_op jit(solution)/shard_map/reduce_sum | solution.py:31
  84.8 0.0 copy-done.2
  84.8 3.6 %fusion.21 = f32[64,1024]{1,0:T(8,128)S(1)} fusion(bf16[8,128,1024]{2,0,1:T(8,128)(2,1)} %all-to-all-done, f32[1024]{0:T(1024)S(1)} %add_rsqrt_fusion, f32[1024]{0:T(1024)S(1)} %broadcast_multiply_fusion, pred[1024]{0:T(1024)(128)(4,1)S(1)} %add_compare_fusion, f32[1,64,1024]{2,1,0:T(8,128)S(1)} %copy-done.2), kind=kOutput, calls=%fused_computation.26 | convolution fusion | flops 810549248 | bytes 2630656 | tf_op jit(solution)/shard_map/nbi,bri->brn/dot_general | solution.py:36
  88.4 5.7 %all-gather = f32[128,1024]{1,0:T(8,128)S(1)} all-gather(f32[64,1024]{1,0:T(8,128)S(1)} %fusion.21), channel_id=2, replica_groups=mesh['blk'=128,'row'=2] {'row'}, dimensions={0}, use_global_device_ids=true | all-gather | bytes 786432 | tf_op jit(solution)/shard_map/all_gather | solution.py:11
  94.1 3.0 %fusion.30 = f32[1,64,1024]{2,1,0:T(8,128)S(1)} fusion(f32[64,1024]{1,0:T(8,128)S(1)} %reduce.18, bf16[8,128,1024]{2,0,1:T(8,128)(2,1)} %all-to-all-done, f32[1024]{0:T(1024)S(1)} %add_rsqrt_fusion, f32[1024]{0:T(1024)S(1)} %broadcast_multiply_fusion, pred[1024]{0:T(1024)(128)(4,1)S(1)} %add_compare_fusion, f32[1,64,1024]{2,1,0:T(8,128)S(1)} %copy-done.2), kind=kOutput, calls=%fused_computation.29 | convolution fusion | flops 810811392 | bytes 2892800 | tf_op jit(solution)/shard_map/nbi,brn->bri/dot_general | solution.py:45
  97.1 0.0 copy-start.1
  97.1 0.4 fusion.34
  97.5 1.9 %all-gather.1 = f32[128,64]{1,0:T(8,128)S(1)} all-gather(f32[64,64]{1,0:T(8,128)S(1)} %fusion.34), channel_id=3, replica_groups=mesh['blk'=128,'row'=2] {'row'}, dimensions={0}, use_global_device_ids=true | all-gather | bytes 49152 | tf_op jit(solution)/shard_map/all_gather | solution.py:11
  99.4 0.1 copy.13
  99.5 0.1 copy.14
  99.6 5.8 %custom-call.8 = f32[1,64,64]{2,1,0:T(8,128)S(1)} custom-call(f32[1,64,64]{2,1,0:T(8,128)S(1)} %fusion.37), custom_call_target="Cholesky" | custom-call | tf_op jit(solution)/shard_map/jit(cholesky)/cholesky | solution.py:59
  105.4 0.6 compare_reduce_fusion
  106.1 1.3 %fusion.39 = (f32[1,64,64]{2,1,0:T(8,128)S(1)}, f32[1,64,64]{2,1,0:T(8,128)}) fusion(f32[1,64,64]{2,1,0:T(8,128)S(1)} %custom-call.8, pred[]{:T(512)} %compare_reduce_fusion), kind=kLoop, calls=%fused_computation.41 | loop fusion | flops 16384 | bytes 49153 | tf_op jit(solution)/shard_map/jit(_solve_triangular)/triangular_solve | solution.py:60
  107.4 4.9 %custom-call.9 = f32[1,64,64]{1,2,0:T(8,128)S(1)} custom-call(f32[1,64,64]{2,1,0:T(8,128)S(1)} %get-tuple-element.3), custom_call_target="InvertDiagBlocksLowerTriangular" | custom-call | tf_op jit(solution)/shard_map/jit(_solve_triangular)/triangular_solve | solution.py:60
  112.3 1.1 %convolution_bitcast_fusion = f32[1,64,1024]{2,1,0:T(8,128)} fusion(f32[1,64,1024]{2,1,0:T(8,128)S(1)} %fusion.30, f32[1,64,64]{1,2,0:T(8,128)S(1)} %custom-call.9), kind=kOutput, calls=%fused_computation.25 | convolution fusion | flops 50331648 | bytes 540672 | tf_op jit(solution)/shard_map/jit(_solve_triangular)/triangular_solve | solution.py:60
  113.4 0.0 copy-done.1
  (7 shorter events, 0.1 us)
Async XLA Ops:
  0.6 1.6 %copy-start = (bf16[8,128,1024]{2,1,0:T(8,128)(2,1)S(1)}, bf16[8,128,1024]{2,1,0:T(8,128)(2,1)}, u32[]{:S(2)}) copy-start(bf16[8,128,1024]{2,1,0:T(8,128)(2,1)} %param.4) | copy-start | bytes 6291460
  14.6 17.2 %copy-start.3 = (s32[128]{0:T(128)S(1)}, s32[128]{0:T(128)}, u32[]{:S(2)}) copy-start(s32[128]{0:T(128)} %param.5) | copy-start | bytes 1540
  14.6 17.8 %copy-start.4 = (s32[128]{0:T(128)S(1)}, s32[128]{0:T(128)}, u32[]{:S(2)}) copy-start(s32[128]{0:T(128)} %param.6) | copy-start | bytes 1540
  14.6 66.0 %all-to-all-start = ((bf16[8,128,1024]{2,0,1:T(8,128)(2,1)}), bf16[8,128,1024]{2,0,1:T(8,128)(2,1)}, u32[]{:S(2)}, u32[]{:S(2)}) async-start(bf16[8,128,1024]{2,0,1:T(8,128)(2,1)} %copy.12), calls=%async_computation | async-start | bytes 4194304 | tf_op jit(solution)/shard_map/all_to_all | solution.py:17
  34.3 50.5 %copy-start.2 = (f32[1,64,1024]{2,1,0:T(8,128)S(1)}, f32[1,64,1024]{2,1,0:T(8,128)}, u32[]{:S(2)}) copy-start(f32[1,64,1024]{2,1,0:T(8,128)} %param.7) | copy-start | bytes 786436
  97.1 16.3 %copy-start.1 = (f32[1,64,1024]{2,1,0:T(8,128)}, f32[1,64,1024]{2,1,0:T(8,128)S(1)}, u32[]{:S(2)}) copy-start(f32[1,64,1024]{2,1,0:T(8,128)S(1)} %fusion.30) | copy-start | bytes 786436
where the time goes:
time: 114 us; the launch traced here: 113 us
  waiting for transfers between devices  46.3 us (41%)
  other arithmetic  22.1 us (19%)
  starting transfers between devices  17.2 us (15%)
  local copies, waits for them, and re-layouts  11.4 us (10%)
  matrix products  8.12 us (7%)
  blocking collectives  7.54 us (7%)
    all_to_all x1, waiting for transfers between devices, body(): lax.all_to_all(ordered, 'blk', split_axis=1, concat_axis=0, tiled=True)  46.3 us
    all_to_all x1, starting transfers between devices, body(): lax.all_to_all(ordered, 'blk', split_axis=1, concat_axis=0, tiled=True)  17.2 us
    gather x1, local copies, waits for them, and re-layouts, body(): ordered = jnp.take(genotypes, assignment, axis=1)  8.06 us
    all_gather x2, blocking collectives, total_of_pieces(): pieces = lax.all_gather(array, axis)  7.54 us
    another operation x3, other arithmetic, body(): factor = jnp.linalg.cholesky(gram_sum)  6.52 us
    another operation x2, other arithmetic, body(): new_basis = jax.scipy.linalg.solve_triangular(factor, image, lower=True)  6.16 us
    dot_general x1, matrix products, body(): jnp.einsum('nbi,bri->brn', standard, basis, precision=lax.Precision.HIGHE...  3.61 us
    dot_general x1, matrix products, body(): jnp.einsum('nbi,brn->bri', standard, projected, precision=lax.Precision.H...  3.02 us
  transfers between devices with their start and end apart: 1, of which 1 were waited for; matrix products, arithmetic and copies ran while one was open for 2% of the time, Pallas kernels for 0%

commit v1 on v0

v1 whole, which is shorter than its diff:
```python
import functools

import jax
import jax.numpy as jnp
from jax import lax
from jax.experimental import pallas as pl
from jax.experimental.pallas import tpu as pltpu
from jax.sharding import PartitionSpec as P

EPS = 1e-05
SHRINK = 0.5
MESH = pl.DeviceIdType.MESH
NX, NZ, NY = 4, 8, 4
PLANE = NX * NY
BLOCKS = NX * NZ * NY
OWN = 8
SAMPLES = BLOCKS * OWN
HALF = 1024
RANK = 64
CHUNK = 256
KX = (1, 2, 3, 0)
PAIRS = ((1, 7), (4,), (2, 6), (3, 5))
BF = jnp.bfloat16
F32 = jnp.float32


def block_of(x, z, y):
    return (x * NZ + z) * NY + y


def remote(src, dst, send_sem, recv_sem, to):
    return pltpu.make_async_remote_copy(
        src_ref=src, dst_ref=dst, send_sem=send_sem, recv_sem=recv_sem,
        device_id=to, device_id_type=MESH,
    )


def split(value):
    high = value.astype(BF)
    low = (value - high.astype(F32)).astype(BF)
    return jnp.concatenate([high, low], axis=0)


def nt(a, b):
    return lax.dot_general(a, b, (((1,), (1,)), ((), ())), preferred_element_type=F32)


def nn(a, b):
    return lax.dot_general(a, b, (((1,), (0,)), ((), ())), preferred_element_type=F32)


def exchange_kernel(
    assign, counts, geno, basis, image_out, gram_out,
    pick, send, zbuf, fin, std, bsplit, pbuf, precv, gbuf, grecv,
    zss, fss, pss, gss, zrs, grs, prs, grr,
):
    me = lax.axis_index("blk")
    row = lax.axis_index("row")
    y = me % NY
    z = (me // NY) % NZ
    x = me // (NY * NZ)
    mate = {"row": 1 - row}
    here = {"blk": me}

    barrier = pltpu.get_barrier_semaphore()
    xs = [(x + k) % NX for k in range(NX)]
    ys = [(y + k) % NY for k in range(NY)]
    peers = [{"blk": block_of(x, (z + d) % NZ, y)} for d in range(1, NZ)]
    peers += [
        {"blk": block_of(xs[i], z, ys[j])} for i in range(NX) for j in range(NY) if i or j
    ]
    peers.append(mate)
    for peer in peers:
        pl.semaphore_signal(barrier, inc=1, device_id=peer, device_id_type=MESH)

    bsplit[...] = split(basis[...])
    gbuf[...] = jnp.zeros_like(gbuf)
    offset = (
        lax.broadcasted_iota(jnp.int32, (OWN, SAMPLES), 1)
        - BLOCKS * lax.broadcasted_iota(jnp.int32, (OWN, SAMPLES), 0)
    )

    def permute(dz):
        zt = (z + dz) % NZ
        for i in range(NX):
            for j in range(NY):
                slot = block_of(xs[KX[i]], zt, j)
                pick[pl.ds((i * NY + j) * OWN, OWN), :] = jnp.where(
                    offset == assign[slot], 1.0, 0.0
                ).astype(BF)
        table = geno[...].reshape(SAMPLES, HALF)
        moved = nn(pick[...], table).astype(BF).reshape(NX, NY, OWN, HALF)
        for i in range(NX):
            send[pl.ds(block_of(xs[KX[i]], zt, 0), NY)] = moved[i]

    def forward(dz, kx):
        for ky in range(NY):
            if kx == 0 and ky == 0:
                continue
            to = block_of(xs[kx], z, ys[ky])
            src = send.at[to] if dz == 0 else zbuf.at[dz, xs[kx], ys[ky]]
            remote(src, fin.at[dz, kx * NY + ky], fss, grs.at[dz], {"blk": to}).start()

    def zsend(dz):
        zt = (z + dz) % NZ
        to = {"blk": block_of(x, zt, y)}
        for kx in KX[:3]:
            remote(
                send.at[pl.ds(block_of(xs[kx], zt, 0), NY)], zbuf.at[dz, xs[kx]],
                zss, zrs.at[dz, kx], to,
            ).start()
        for ky in (1, 2, 3):
            remote(
                send.at[block_of(x, zt, ys[ky])], zbuf.at[dz, x, ys[ky]],
                zss, zrs.at[dz, 0], to,
            ).start()
        remote(send.at[block_of(x, zt, y)], fin.at[dz, 0], zss, grs.at[dz], to).start()

    def wait_z(dz, kx):
        part = zbuf.at[dz, 0, pl.ds(0, 3)] if kx == 0 else zbuf.at[dz, 0]
        remote(part, part, zss, zrs.at[dz, kx], here).wait_recv()

    for step, dz in enumerate((1, 7, 0, 4, 2, 6, 3, 5)):
        permute(dz)
        if step == 0:
            pl.semaphore_wait(barrier, len(peers))
        if dz == 0:
            for kx in KX:
                forward(0, kx)
            fin[0, 0] = send[me]
        else:
            zsend(dz)

    def wait_group(dz):
        part = fin.at[0, pl.ds(1, PLANE - 1)] if dz == 0 else fin.at[dz]
        remote(part, part, fss, grs.at[dz], here).wait_recv()

    rows = PLANE * OWN
    wait_group(0)
    shift = jnp.zeros((OWN, HALF), F32)
    for i in range(PLANE):
        shift += fin[0, i].astype(F32)
    shift = jnp.sum(shift, axis=0, keepdims=True) * (1.0 / rows)

    def add_group(dz, carry):
        def one(i, carry):
            total, square = carry
            d = fin[dz, i].astype(F32) - shift
            return total + d, square + d * d

        return lax.fori_loop(0, PLANE, one, carry, unroll=4)

    zero = jnp.zeros((OWN, HALF), F32)
    carry = add_group(0, (zero, zero))
    late = ()
    for pair in PAIRS:
        for kx in KX:
            for dz in pair:
                wait_z(dz, kx)
                forward(dz, kx)
        for dz in late:
            wait_group(dz)
            carry = add_group(dz, carry)
        late = pair
    for dz in late:
        wait_group(dz)
        carry = add_group(dz, carry)

    first = jnp.sum(carry[0], axis=0, keepdims=True) * (1.0 / SAMPLES)
    second = jnp.sum(carry[1], axis=0, keepdims=True) * (1.0 / SAMPLES)
    mean = shift + first
    var = second - first * first
    live = counts[assign[me]]
    column = lax.broadcasted_iota(jnp.int32, (1, HALF), 1) + row * HALF
    mask = jnp.where(column < live, 1.0, 0.0)
    scale = lax.rsqrt(var + EPS) * mask

    copies = []
    groups = CHUNK // rows
    for c in range(SAMPLES // CHUNK):
        part = fin[pl.ds(c * groups, groups)].reshape(CHUNK, HALF)
        part = ((part.astype(F32) - mean) * scale).astype(BF)
        std[c] = part
        both = nt(bsplit[...], part)
        pbuf[c] = both[:RANK] + both[RANK:]
        copy = remote(pbuf.at[c], precv.at[c], pss.at[c], prs.at[c], mate)
        copy.start()
        copies.append(copy)
    acc = jnp.zeros((2 * RANK, HALF), F32)
    for c in range(SAMPLES // CHUNK):
        copies[c].wait_recv()
        acc += nn(split(pbuf[c] + precv[c]), std[c])
    product = acc[:RANK] + acc[RANK:]
    image = product * (SHRINK / SAMPLES) + (1.0 - SHRINK) * (basis[...] * mask)
    image_out[...] = image
    halves = split(image)
    outer = nt(halves, halves[:RANK]) + nt(halves, halves[RANK:])
    gbuf[:, pl.ds(0, RANK)] = outer[:RANK] + outer[RANK:]
    swap = remote(gbuf, grecv, gss, grr, mate)
    swap.start()
    for copy in copies:
        copy.wait_send()
    for dz in range(NZ):
        part = fin.at[dz, pl.ds(1, PLANE - 1)]
        remote(part, part, fss, grs.at[dz], here).wait_send()
    part = send.at[pl.ds(0, (NZ - 1) * PLANE)]
    remote(part, part, zss, grs.at[0], here).wait_send()
    swap.wait_recv()
    gram_out[...] = gbuf[...] + grecv[...]
    swap.wait_send()


def spread(row, n):
    return jnp.broadcast_to(row, (n, row.shape[1]))


def factor_kernel(image_in, gram, image_out, basis_out, factor_out):
    wide = 2 * RANK
    image = image_in[...]
    image_out[...] = image
    lane = lax.broadcasted_iota(jnp.int32, (RANK, wide), 1)
    line = lax.broadcasted_iota(jnp.int32, (RANK, wide), 0)
    work = jnp.where(lane < RANK, gram[...], jnp.where(lane == line + RANK, 1.0, 0.0))
    tiles = [work[8 * b : 8 * b + 8] for b in range(8)]
    below = lax.broadcasted_iota(jnp.int32, (8, wide), 0)
    done = []
    for p in range(8):
        cols = {
            (c, b): jnp.broadcast_to(tiles[b][:, 8 * p + c : 8 * p + c + 1], (8, wide))
            for c in range(8)
            for b in range(p, 8)
        }
        finished = jnp.zeros((8, wide), F32)
        for c in range(8):
            inv = lax.rsqrt(spread(cols[c, p][c : c + 1], 8))
            line_c = spread(tiles[p][c : c + 1], 8) * inv
            finished = jnp.where(below == c, line_c, finished)
            lows = [cols[c, b] * inv for b in range(p, 8)]
            for d in range(c + 1, 8):
                factor = spread(lows[0][d : d + 1], 8)
                for b in range(p, 8):
                    cols[d, b] = cols[d, b] - lows[b - p] * factor
            for b in range(p, 8):
                tiles[b] = tiles[b] - lows[b - p] * line_c
        done.append(finished)
    full = jnp.concatenate(done, axis=0)
    upper = jnp.where((lane < RANK) & (lane >= line), full, 0.0)
    factor_out[...] = jnp.transpose(upper[:, :RANK])
    inverse = jnp.where((lane >= RANK) & (lane - RANK <= line), full, 0.0)
    both = split(inverse)
    halves = split(image)
    high = jnp.concatenate([halves[:RANK], halves[:RANK]], axis=0)
    low = jnp.concatenate([halves[RANK:], halves[RANK:]], axis=0)
    one = nn(both, high)
    two = nn(both[:RANK], low)
    basis_out[...] = one[:RANK] + one[RANK:] + two


def body(genotypes, assignment, snp_counts, basis):
    vmem = pl.BlockSpec(memory_space=pltpu.VMEM)
    smem = pl.BlockSpec(memory_space=pltpu.SMEM)
    dma = pltpu.SemaphoreType.DMA
    chunks = SAMPLES // CHUNK
    image, gram = pl.pallas_call(
        exchange_kernel,
        out_shape=(
            jax.ShapeDtypeStruct((RANK, HALF), F32),
            jax.ShapeDtypeStruct((RANK, 2 * RANK), F32),
        ),
        in_specs=[smem, smem, vmem, vmem],
        out_specs=(vmem, vmem),
        scratch_shapes=[
            pltpu.VMEM((PLANE * OWN, SAMPLES), BF),
            pltpu.VMEM((BLOCKS, OWN, HALF), BF),
            pltpu.VMEM((NZ, NX, NY, OWN, HALF), BF),
            pltpu.VMEM((NZ, PLANE, OWN, HALF), BF),
            pltpu.VMEM((chunks, CHUNK, HALF), BF),
            pltpu.VMEM((2 * RANK, HALF), BF),
            pltpu.VMEM((chunks, RANK, CHUNK), F32),
            pltpu.VMEM((chunks, RANK, CHUNK), F32),
            pltpu.VMEM((RANK, 2 * RANK), F32),
            pltpu.VMEM((RANK, 2 * RANK), F32),
            dma, dma, dma((chunks,)), dma,
            dma((NZ, NX)), dma((NZ,)), dma((chunks,)), dma,
        ],
        compiler_params=pltpu.CompilerParams(
            collective_id=0, has_side_effects=True, vmem_limit_bytes=32 << 20
        ),
        name="exchange",
    )(assignment, snp_counts, genotypes, basis.reshape(RANK, HALF))
    image, new_basis, factor = pl.pallas_call(
        factor_kernel,
        out_shape=(
            jax.ShapeDtypeStruct((RANK, HALF), F32),
            jax.ShapeDtypeStruct((RANK, HALF), F32),
            jax.ShapeDtypeStruct((RANK, RANK), F32),
        ),
        in_specs=[vmem, vmem],
        out_specs=(vmem, vmem, vmem),
        compiler_params=pltpu.CompilerParams(vmem_limit_bytes=8 << 20),
        name="factorize",
    )(image, gram)
    return image[None], new_basis[None], factor[None]


def solution(mesh):
    in_specs = (P("blk", None, "row"), P(), P(), P("blk", None, "row"))
    out_specs = (P("blk", None, "row"), P("blk", None, "row"), P("blk", None, None))
    return jax.shard_map(body, mesh=mesh, in_specs=in_specs, out_specs=out_specs, check_vma=False)
```

time: 114 us -> 74.7 us (0.66)
  Pallas kernels: 0 us -> 70 us
  waiting for transfers between devices: 46.3 us -> 0 us
  other arithmetic: 22.1 us -> 0 us
  starting transfers between devices: 17.2 us -> 0 us
  matrix products: 8.12 us -> 0 us
  local copies, waits for them, and re-layouts: 11.4 us -> 3.84 us
  blocking collectives: 7.54 us -> 0 us
    pallas_call x0 -> x2, Pallas kernels: none -> 70 us  [the longest x1 67.4 us: body(): pl.pallas_call(exchange_kernel, out_shape=(jax.ShapeDtypeStruct((RANK, HA...]
    all_to_all x1 -> x0, waiting for transfers between devices: 46.3 us -> none  [body(): lax.all_to_all(ordered, 'blk', split_axis=1, concat_axis=0, tiled=True)]
    all_to_all x1 -> x0, starting transfers between devices: 17.2 us -> none  [body(): lax.all_to_all(ordered, 'blk', split_axis=1, concat_axis=0, tiled=True)]
    another operation x5 -> x0, other arithmetic: 12.7 us -> none  [the longest x3 6.52 us: body(): factor = jnp.linalg.cholesky(gram_sum)]
    gather x1 -> x0, local copies, waits for them, and re-layouts: 8.06 us -> none  [body(): ordered = jnp.take(genotypes, assignment, axis=1)]
    all_gather x2 -> x0, blocking collectives: 7.54 us -> none  [total_of_pieces(): pieces = lax.all_gather(array, axis)]
    dot_general x3 -> x0, matrix products: 6.98 us -> none  [the longest x1 3.61 us: body(): jnp.einsum('nbi,bri->brn', standard, basis, precision=lax.Precision.HIGHE...]
    reduce_sum x5 -> x0, other arithmetic: 5.47 us -> none  [the longest x1 2.19 us: body(): col_var = jnp.mean(centered * centered, axis=0)]
  transfers between devices with their start and end apart: 1 -> 0, of which waited for: 1 -> 0; matrix products, arithmetic and copies ran while one was open for 2% -> 0% of each run, Pallas kernels for 0% -> 0%
where the time goes in v1:
time: 74.7 us; the launch traced here: 74.5 us
  Pallas kernels  70 us (94%)
  local copies, waits for them, and re-layouts  3.84 us (5%)
    pallas_call x1, Pallas kernels, body(): pl.pallas_call(exchange_kernel, out_shape=(jax.ShapeDtypeStruct((RANK, HA...  67.4 us
    unnamed x8, local copies, waits for them, and re-layouts  3.84 us
    pallas_call x1, Pallas kernels, body(): pl.pallas_call(factor_kernel, out_shape=(jax.ShapeDtypeStruct((RANK, HALF...  2.64 us

profile of v1, /device:TPU:1, one launch (start us, length us, event | category | flops | bytes accessed | tf_op | source)
XLA Modules:
  0.0 74.5 jit_solution(12556928832633025332)
XLA Ops:
  0.6 0.0 copy-start
  0.6 1.6 %copy-done = bf16[8,128,1024]{2,1,0:T(8,128)(2,1)S(1)} copy-done((bf16[8,128,1024]{2,1,0:T(8,128)(2,1)S(1)}, bf16[8,128,1024]{2,1,0:T(8,128)(2,1)}, u32[]{:S(2)}) %copy-start) | copy-done | bytes 2097176
  2.2 0.0 copy-start.1
  2.2 0.9 %copy-done.1 = f32[1,64,1024]{2,1,0:T(8,128)S(1)} copy-done((f32[1,64,1024]{2,1,0:T(8,128)S(1)}, f32[1,64,1024]{2,1,0:T(8,128)}, u32[]{:S(2)}) %copy-start.1) | copy-done | bytes 262168
  3.2 0.0 copy-start.2
  3.2 0.7 copy-done.2
  3.8 0.0 copy-start.3
  3.8 0.7 copy-done.3
  4.5 67.4 %exchange.1 = (f32[64,1024]{1,0:T(8,128)S(1)}, f32[64,128]{1,0:T(8,128)S(1)}) custom-call(s32[128]{0:T(128)S(1)} %copy-done.2, s32[128]{0:T(128)S(1)} %copy-done.3, bf16[8,128,1024]{2,1,0:T(8,128)(2,1)S(1)} %copy-done, f32[64,1024]{1,0:T(8,128)S(1)} %bitcast.4), custom_call_target="tpu_custom_call" | custom-call | tf_op jit(solution)/shard_map/exchange/pallas_call | solution.py:264
  71.9 2.6 %factorize.1 = (f32[64,1024]{1,0:T(8,128)}, f32[64,1024]{1,0:T(8,128)}, f32[64,64]{1,0:T(8,128)}) custom-call(f32[64,1024]{1,0:T(8,128)S(1)} %get-tuple-element.8.image_in, f32[64,128]{1,0:T(8,128)S(1)} %get-tuple-element.9.gram), custom_call_target="tpu_custom_call" | custom-call | tf_op jit(solution)/shard_map/factorize/pallas_call | solution.py:291
Async XLA Ops:
  0.6 1.6 %copy-start = (bf16[8,128,1024]{2,1,0:T(8,128)(2,1)S(1)}, bf16[8,128,1024]{2,1,0:T(8,128)(2,1)}, u32[]{:S(2)}) copy-start(bf16[8,128,1024]{2,1,0:T(8,128)(2,1)} %geno.1) | copy-start | bytes 6291460
  2.2 0.9 %copy-start.1 = (f32[1,64,1024]{2,1,0:T(8,128)S(1)}, f32[1,64,1024]{2,1,0:T(8,128)}, u32[]{:S(2)}) copy-start(f32[1,64,1024]{2,1,0:T(8,128)} %param.7) | copy-start | bytes 786436
  3.2 0.7 copy-start.2
  3.8 0.7 copy-start.3

commit v2 on v1

--- a/solution.py
+++ b/solution.py
@@ -19,7 +19,7 @@
 RANK = 64
 CHUNK = 256
 KX = (1, 2, 3, 0)
-PAIRS = ((1, 7), (4,), (2, 6), (3, 5))
+ORDER = (4, 3, 5, 2, 6, 1, 7, 0)
 BF = jnp.bfloat16
 F32 = jnp.float32
 
@@ -50,9 +50,9 @@
 
 
 def exchange_kernel(
-    assign, counts, geno, basis, image_out, gram_out,
-    pick, send, zbuf, fin, std, bsplit, pbuf, precv, gbuf, grecv,
-    zss, fss, pss, gss, zrs, grs, prs, grr,
+    assign_in, counts_in, geno_in, basis_in, image_out, gram_out,
+    assign, counts, geno, basis, pick, send, zbuf, fin, std, bsplit, pbuf, precv, gbuf, grecv,
+    load_sem, zss, fss, pss, gss, zrs, grs, prs, grr,
 ):
     me = lax.axis_index("blk")
     row = lax.axis_index("row")
@@ -62,6 +62,14 @@
     mate = {"row": 1 - row}
     here = {"blk": me}
 
+    loads = [
+        pltpu.make_async_copy(src, dst, load_sem.at[i])
+        for i, (src, dst) in enumerate(
+            ((assign_in, assign), (geno_in, geno), (basis_in, basis), (counts_in, counts))
+        )
+    ]
+    for load in loads:
+        load.start()
     barrier = pltpu.get_barrier_semaphore()
     xs = [(x + k) % NX for k in range(NX)]
     ys = [(y + k) % NY for k in range(NY)]
@@ -73,98 +81,126 @@
     for peer in peers:
         pl.semaphore_signal(barrier, inc=1, device_id=peer, device_id_type=MESH)
 
-    bsplit[...] = split(basis[...])
     gbuf[...] = jnp.zeros_like(gbuf)
     offset = (
         lax.broadcasted_iota(jnp.int32, (OWN, SAMPLES), 1)
         - BLOCKS * lax.broadcasted_iota(jnp.int32, (OWN, SAMPLES), 0)
     )
 
-    def permute(dz):
-        zt = (z + dz) % NZ
-        for i in range(NX):
+    loads[0].wait()
+
+    def permute(kx, half):
+        column = (x + kx) % NX
+        planes = []
+        for i in range(4):
+            dz = jnp.where(half == 0, ORDER[i], ORDER[4 + i])
+            planes.append((dz, (z + dz) % NZ))
+        for i, (_, zt) in enumerate(planes):
             for j in range(NY):
-                slot = block_of(xs[KX[i]], zt, j)
+                slot = block_of(column, zt, j)
                 pick[pl.ds((i * NY + j) * OWN, OWN), :] = jnp.where(
                     offset == assign[slot], 1.0, 0.0
                 ).astype(BF)
         table = geno[...].reshape(SAMPLES, HALF)
-        moved = nn(pick[...], table).astype(BF).reshape(NX, NY, OWN, HALF)
-        for i in range(NX):
-            send[pl.ds(block_of(xs[KX[i]], zt, 0), NY)] = moved[i]
-
-    def forward(dz, kx):
-        for ky in range(NY):
-            if kx == 0 and ky == 0:
-                continue
-            to = block_of(xs[kx], z, ys[ky])
-            src = send.at[to] if dz == 0 else zbuf.at[dz, xs[kx], ys[ky]]
-            remote(src, fin.at[dz, kx * NY + ky], fss, grs.at[dz], {"blk": to}).start()
-
-    def zsend(dz):
+        moved = nn(pick[...], table).astype(BF).reshape(4, NY, OWN, HALF)
+        for i, (_, zt) in enumerate(planes):
+            send[pl.ds(block_of(column, zt, 0), NY)] = moved[i]
+        return column, planes
+
+    def forward(dz, kx, column, src):
+        def one(ky):
+            yt = ys[ky]
+            to = block_of(column, z, yt)
+            remote(src(to, yt), fin.at[kx * NY + ky, dz], fss, grs.at[kx], {"blk": to}).start()
+
+        for ky in range(1, NY):
+            one(ky)
+        if isinstance(kx, int):
+            if kx:
+                one(0)
+        else:
+            pl.when(kx > 0)(lambda: one(0))
+
+    def from_send(to, yt):
+        return send.at[to]
+
+    def push(i, _):
+        kx, half = (i // 2 + 1) % NX, i % 2
+        pl.when(i == 0)(loads[1].wait)
+        column, planes = permute(kx, half)
+        pl.when(i == 0)(lambda: pl.semaphore_wait(barrier, len(peers)))
+        for j, (dz, zt) in enumerate(planes):
+            to = {"blk": block_of(x, zt, y)}
+
+            def whole():
+                remote(
+                    send.at[pl.ds(block_of(column, zt, 0), NY)], zbuf.at[dz, kx],
+                    zss, zrs.at[dz, kx], to,
+                ).start()
+
+            def three():
+                for ky in range(1, NY):
+                    remote(
+                        send.at[block_of(x, zt, ys[ky])], zbuf.at[dz, 0, ys[ky]],
+                        zss, zrs.at[dz, 0], to,
+                    ).start()
+
+            def either():
+                pl.when(kx > 0)(whole)
+                pl.when(kx == 0)(three)
+
+            if j < 3:
+                either()
+            else:
+                pl.when(half == 0)(either)
+                pl.when(half == 1)(lambda: forward(0, kx, column, from_send))
+        return 0
+
+    lax.fori_loop(0, 8, push, 0)
+    for dz in ORDER[:7]:
         zt = (z + dz) % NZ
-        to = {"blk": block_of(x, zt, y)}
-        for kx in KX[:3]:
-            remote(
-                send.at[pl.ds(block_of(xs[kx], zt, 0), NY)], zbuf.at[dz, xs[kx]],
-                zss, zrs.at[dz, kx], to,
-            ).start()
-        for ky in (1, 2, 3):
-            remote(
-                send.at[block_of(x, zt, ys[ky])], zbuf.at[dz, x, ys[ky]],
-                zss, zrs.at[dz, 0], to,
-            ).start()
-        remote(send.at[block_of(x, zt, y)], fin.at[dz, 0], zss, grs.at[dz], to).start()
-
-    def wait_z(dz, kx):
-        part = zbuf.at[dz, 0, pl.ds(0, 3)] if kx == 0 else zbuf.at[dz, 0]
-        remote(part, part, zss, zrs.at[dz, kx], here).wait_recv()
-
-    for step, dz in enumerate((1, 7, 0, 4, 2, 6, 3, 5)):
-        permute(dz)
-        if step == 0:
-            pl.semaphore_wait(barrier, len(peers))
-        if dz == 0:
-            for kx in KX:
-                forward(0, kx)
-            fin[0, 0] = send[me]
-        else:
-            zsend(dz)
-
-    def wait_group(dz):
-        part = fin.at[0, pl.ds(1, PLANE - 1)] if dz == 0 else fin.at[dz]
-        remote(part, part, fss, grs.at[dz], here).wait_recv()
-
-    rows = PLANE * OWN
-    wait_group(0)
-    shift = jnp.zeros((OWN, HALF), F32)
-    for i in range(PLANE):
-        shift += fin[0, i].astype(F32)
-    shift = jnp.sum(shift, axis=0, keepdims=True) * (1.0 / rows)
-
-    def add_group(dz, carry):
+        to = block_of(x, zt, y)
+        remote(send.at[to], fin.at[0, dz], zss, grs.at[4], {"blk": to}).start()
+    fin[0, 0] = send[me]
+    loads[2].wait()
+    loads[3].wait()
+    bsplit[...] = split(basis[...])
+
+    def wait_group(part, sem):
+        remote(part, part, fss, grs.at[sem], here).wait_recv()
+
+    def add_rows(first_slot, count, shift, carry):
         def one(i, carry):
             total, square = carry
-            d = fin[dz, i].astype(F32) - shift
+            d = fin[first_slot + i // NZ, i % NZ].astype(F32) - shift
             return total + d, square + d * d
 
-        return lax.fori_loop(0, PLANE, one, carry, unroll=4)
+        return lax.fori_loop(0, count, one, carry, unroll=4)
 
     zero = jnp.zeros((OWN, HALF), F32)
-    carry = add_group(0, (zero, zero))
-    late = ()
-    for pair in PAIRS:
-        for kx in KX:
-            for dz in pair:
-                wait_z(dz, kx)
-                forward(dz, kx)
-        for dz in late:
-            wait_group(dz)
-            carry = add_group(dz, carry)
-        late = pair
-    for dz in late:
-        wait_group(dz)
-        carry = add_group(dz, carry)
+    shift, carry = None, (zero, zero)
+    for step, kx in enumerate(KX):
+        for dz in ORDER[:7]:
+            part = zbuf.at[dz, 0, pl.ds(0, 3)] if kx == 0 else zbuf.at[dz, 0]
+            remote(part, part, zss, zrs.at[dz, kx], here).wait_recv()
+            forward(dz, kx, xs[kx], lambda to, yt: zbuf.at[dz, kx, yt])
+        if step == 0:
+            continue
+        prev = KX[step - 1]
+        wait_group(fin.at[pl.ds(prev * NY, NY)], prev)
+        if step == 1:
+            rows = NY * NZ
+
+            def one(i, total):
+                return total + fin[NY + i // NZ, i % NZ].astype(F32)
+
+            shift = lax.fori_loop(0, rows, one, zero, unroll=4)
+            shift = jnp.sum(shift, axis=0, keepdims=True) * (1.0 / (rows * OWN))
+        carry = add_rows(prev * NY, NY * NZ, shift, carry)
+    wait_group(fin.at[pl.ds(1, NY - 1)], 0)
+    carry = add_rows(1, (NY - 1) * NZ, shift, carry)
+    wait_group(fin.at[0, pl.ds(1, NZ - 1)], 4)
+    carry = add_rows(0, NZ, shift, carry)
 
     first = jnp.sum(carry[0], axis=0, keepdims=True) * (1.0 / SAMPLES)
     second = jnp.sum(carry[1], axis=0, keepdims=True) * (1.0 / SAMPLES)
@@ -175,19 +211,17 @@
     mask = jnp.where(column < live, 1.0, 0.0)
     scale = lax.rsqrt(var + EPS) * mask
 
-    copies = []
-    groups = CHUNK // rows
-    for c in range(SAMPLES // CHUNK):
-        part = fin[pl.ds(c * groups, groups)].reshape(CHUNK, HALF)
+    copies = {}
+    for c in KX:
+        part = fin[pl.ds(c * NY, NY)].reshape(CHUNK, HALF)
         part = ((part.astype(F32) - mean) * scale).astype(BF)
         std[c] = part
         both = nt(bsplit[...], part)
         pbuf[c] = both[:RANK] + both[RANK:]
-        copy = remote(pbuf.at[c], precv.at[c], pss.at[c], prs.at[c], mate)
-        copy.start()
-        copies.append(copy)
+        copies[c] = remote(pbuf.at[c], precv.at[c], pss.at[c], prs.at[c], mate)
+        copies[c].start()
     acc = jnp.zeros((2 * RANK, HALF), F32)
-    for c in range(SAMPLES // CHUNK):
+    for c in KX:
         copies[c].wait_recv()
         acc += nn(split(pbuf[c] + precv[c]), std[c])
     product = acc[:RANK] + acc[RANK:]
@@ -198,11 +232,11 @@
     gbuf[:, pl.ds(0, RANK)] = outer[:RANK] + outer[RANK:]
     swap = remote(gbuf, grecv, gss, grr, mate)
     swap.start()
-    for copy in copies:
-        copy.wait_send()
+    for c in KX:
+        copies[c].wait_send()
     for dz in range(NZ):
-        part = fin.at[dz, pl.ds(1, PLANE - 1)]
-        remote(part, part, fss, grs.at[dz], here).wait_send()
+        part = fin.at[pl.ds(1, PLANE - 1), dz]
+        remote(part, part, fss, grs.at[0], here).wait_send()
     part = send.at[pl.ds(0, (NZ - 1) * PLANE)]
     remote(part, part, zss, grs.at[0], here).wait_send()
     swap.wait_recv()
@@ -258,7 +292,7 @@
 
 def body(genotypes, assignment, snp_counts, basis):
     vmem = pl.BlockSpec(memory_space=pltpu.VMEM)
-    smem = pl.BlockSpec(memory_space=pltpu.SMEM)
+    hbm = pl.BlockSpec(memory_space=pltpu.HBM)
     dma = pltpu.SemaphoreType.DMA
     chunks = SAMPLES // CHUNK
     image, gram = pl.pallas_call(
@@ -267,27 +301,34 @@
             jax.ShapeDtypeStruct((RANK, HALF), F32),
             jax.ShapeDtypeStruct((RANK, 2 * RANK), F32),
         ),
-        in_specs=[smem, smem, vmem, vmem],
+        in_specs=[hbm] * 4,
         out_specs=(vmem, vmem),
         scratch_shapes=[
+            pltpu.SMEM((BLOCKS,), jnp.int32),
+            pltpu.SMEM((BLOCKS,), jnp.int32),
+            pltpu.VMEM((OWN, BLOCKS, HALF), BF),
+            pltpu.VMEM((RANK, HALF), F32),
             pltpu.VMEM((PLANE * OWN, SAMPLES), BF),
             pltpu.VMEM((BLOCKS, OWN, HALF), BF),
             pltpu.VMEM((NZ, NX, NY, OWN, HALF), BF),
-            pltpu.VMEM((NZ, PLANE, OWN, HALF), BF),
+            pltpu.VMEM((PLANE, NZ, OWN, HALF), BF),
             pltpu.VMEM((chunks, CHUNK, HALF), BF),
             pltpu.VMEM((2 * RANK, HALF), BF),
             pltpu.VMEM((chunks, RANK, CHUNK), F32),
             pltpu.VMEM((chunks, RANK, CHUNK), F32),
             pltpu.VMEM((RANK, 2 * RANK), F32),
             pltpu.VMEM((RANK, 2 * RANK), F32),
-            dma, dma, dma((chunks,)), dma,
-            dma((NZ, NX)), dma((NZ,)), dma((chunks,)), dma,
+            dma((4,)), dma, dma, dma((chunks,)), dma,
+            dma((NZ, NX)), dma((5,)), dma((chunks,)), dma,
         ],
         compiler_params=pltpu.CompilerParams(
             collective_id=0, has_side_effects=True, vmem_limit_bytes=32 << 20
         ),
         name="exchange",
-    )(assignment, snp_counts, genotypes, basis.reshape(RANK, HALF))
+    )(*(
+        pltpu.with_memory_space_constraint(a, pltpu.HBM)
+        for a in (assignment, snp_counts, genotypes, basis.reshape(RANK, HALF))
+    ))
     image, new_basis, factor = pl.pallas_call(
         factor_kernel,
         out_shape=(

time: 74.7 us -> 68.5 us (0.917)
  local copies, waits for them, and re-layouts: 3.84 us -> 0 us
  Pallas kernels: 70 us -> 67.8 us
    unnamed x8 -> x0, local copies, waits for them, and re-layouts: 3.84 us -> none
    pallas_call x1, Pallas kernels: 67.4 us -> 65.1 us  [body(): pl.pallas_call(exchange_kernel, out_shape=(jax.ShapeDtypeStruct((RANK, HA...]
where the time goes in v2:
time: 68.5 us; the launch traced here: 68.4 us
  Pallas kernels  67.8 us (99%)
    pallas_call x1, Pallas kernels, body(): pl.pallas_call(exchange_kernel, out_shape=(jax.ShapeDtypeStruct((RANK, HA...  65.1 us
    pallas_call x1, Pallas kernels, body(): pl.pallas_call(factor_kernel, out_shape=(jax.ShapeDtypeStruct((RANK, HALF...  2.64 us

profile of v2, /device:TPU:1, one launch (start us, length us, event | category | flops | bytes accessed | tf_op | source)
XLA Modules:
  0.0 68.4 jit_solution(11642366832980110188)
XLA Ops:
  0.6 65.1 %exchange.1 = (f32[64,1024]{1,0:T(8,128)S(1)}, f32[64,128]{1,0:T(8,128)S(1)}) custom-call(s32[128]{0:T(128)} %assign_in.1, s32[128]{0:T(128)} %counts_in.1, bf16[8,128,1024]{2,1,0:T(8,128)(2,1)} %geno_in.1, f32[64,1024]{1,0:T(8,128)} %bitcast.4), custom_call_target="tpu_custom_call" | custom-call | tf_op jit(solution)/shard_map/exchange/pallas_call | solution.py:298
  65.8 2.6 %factorize.1 = (f32[64,1024]{1,0:T(8,128)}, f32[64,1024]{1,0:T(8,128)}, f32[64,64]{1,0:T(8,128)}) custom-call(f32[64,1024]{1,0:T(8,128)S(1)} %get-tuple-element.8.image_in, f32[64,128]{1,0:T(8,128)S(1)} %get-tuple-element.9.gram), custom_call_target="tpu_custom_call" | custom-call | tf_op jit(solution)/shard_map/factorize/pallas_call | solution.py:332

commit v3 on v2

--- a/solution.py
+++ b/solution.py
@@ -248,10 +248,11 @@
     return jnp.broadcast_to(row, (n, row.shape[1]))
 
 
-def factor_kernel(image_in, gram, image_out, basis_out, factor_out):
+def factor_kernel(image_in, gram, image_out, basis_out, factor_out, sem):
     wide = 2 * RANK
     image = image_in[...]
-    image_out[...] = image
+    copy = pltpu.make_async_copy(image_in, image_out, sem)
+    copy.start()
     lane = lax.broadcasted_iota(jnp.int32, (RANK, wide), 1)
     line = lax.broadcasted_iota(jnp.int32, (RANK, wide), 0)
     work = jnp.where(lane < RANK, gram[...], jnp.where(lane == line + RANK, 1.0, 0.0))
@@ -288,6 +289,7 @@
     one = nn(both, high)
     two = nn(both[:RANK], low)
     basis_out[...] = one[:RANK] + one[RANK:] + two
+    copy.wait()
 
 
 def body(genotypes, assignment, snp_counts, basis):
@@ -337,7 +339,8 @@
             jax.ShapeDtypeStruct((RANK, RANK), F32),
         ),
         in_specs=[vmem, vmem],
-        out_specs=(vmem, vmem, vmem),
+        out_specs=(hbm, vmem, vmem),
+        scratch_shapes=[dma],
         compiler_params=pltpu.CompilerParams(vmem_limit_bytes=8 << 20),
         name="factorize",
     )(image, gram)

time: 68.5 us -> 68.5 us (level)
  no operation moved by 1% of the time
where the time goes in v3:
time: 68.5 us; the launch traced here: 68.4 us
  Pallas kernels  67.8 us (99%)
    pallas_call x1, Pallas kernels, body(): pl.pallas_call(exchange_kernel, out_shape=(jax.ShapeDtypeStruct((RANK, HA...  65.1 us
    pallas_call x1, Pallas kernels, body(): pl.pallas_call(factor_kernel, out_shape=(jax.ShapeDtypeStruct((RANK, HALF...  2.65 us

profile of v3, /device:TPU:1, one launch (start us, length us, event | category | flops | bytes accessed | tf_op | source)
XLA Modules:
  0.0 68.4 jit_solution(16397482818832971873)
XLA Ops:
  0.6 65.1 %exchange.1 = (f32[64,1024]{1,0:T(8,128)S(1)}, f32[64,128]{1,0:T(8,128)S(1)}) custom-call(s32[128]{0:T(128)} %assign_in.1, s32[128]{0:T(128)} %counts_in.1, bf16[8,128,1024]{2,1,0:T(8,128)(2,1)} %geno_in.1, f32[64,1024]{1,0:T(8,128)} %bitcast.4), custom_call_target="tpu_custom_call" | custom-call | tf_op jit(solution)/shard_map/exchange/pallas_call | solution.py:300
  65.8 2.7 %factorize.1 = (f32[64,1024]{1,0:T(8,128)}, f32[64,1024]{1,0:T(8,128)}, f32[64,64]{1,0:T(8,128)}) custom-call(f32[64,1024]{1,0:T(8,128)S(1)} %get-tuple-element.8.image_in, f32[64,128]{1,0:T(8,128)S(1)} %get-tuple-element.9.gram), custom_call_target="tpu_custom_call" | custom-call | tf_op jit(solution)/shard_map/factorize/pallas_call | solution.py:334
